TPU v7x, 32 devices: a whole 2x2x4 slice. The times are simulated.
32 devices in a mesh: groups: 2 (over x), seq: 8 (over z, y), expert: 2 (over core).
Axes of the slice: x: 2, y: 2, z: 4, core: 2. Of those that a mesh axis runs over, the one named last changes fastest.
Arguments:
- residual: bfloat16 [8, 6144], P('groups', 'seq'), parts along dimension 0, may hold values from -27 to 27
- queries: bfloat16 [8, 6144], P('groups', 'expert'), parts along dimension 0, may hold values from -6 to 6
- new_entries: bfloat16 [2, 8, 1024], P(None, 'groups', 'expert'), parts along dimension 1, may hold values from -6 to 6
- kv_cache: bfloat16 [2, 1024, 16384], P(None, 'seq', ('groups', 'expert')), parts along dimension 2, may hold values from -6 to 6
- lengths: int32 [8], P('groups'), parts along dimension 0, may hold values from 128 to 2048, as said below
- routing: int32 [8, 2], P('groups'), parts along dimension 0, may hold values from 0 to 3, all different within a row
- w_out: bfloat16 [6144, 6144], P('expert', 'seq'), may hold values from -0.5 to 0.5
- norm_gain: bfloat16 [6144], replicated, may hold values from 0.5 to 1.5
- router: bfloat16 [6144, 4], replicated, may hold values from -0.078125 to 0.078125
- w_gate: bfloat16 [4, 6144, 1024], P('expert', None, 'seq'), may hold values from -0.078125 to 0.078125
- w_up: bfloat16 [4, 6144, 1024], P('expert', None, 'seq'), may hold values from -0.078125 to 0.078125
- w_down: bfloat16 [4, 1024, 6144], P('expert', 'seq'), may hold values from -0.75 to 0.75
Outputs:
- attended: bfloat16 [8, 6144], P('groups', 'seq'), parts along dimension 0
- expert_out: bfloat16 [8, 6144], P('groups', 'seq'), parts along dimension 0
There are 2 independent parts, one for each index of `groups`. A program takes and returns all parts, laid end to end along the dimension named above; an argument that names none is the same for every part. Nothing has to cross between parts.
Inputs may be any that keep to these rules, and one draw needn't show every extreme that they name: `lengths`: every draw has a request of exactly 2048 positions. `routing`: each request names two different experts.
All inputs are finite; a program needn't handle non-finite values.
Results may differ from a plain program's by a relative error of at most 0.02.
Values may be sent and summed in bfloat16 or wider, within the bound.
A program may use at most 128 MiB of HBM per device.

v0:
```python
import math
import jax
import jax.numpy as jnp
from jax import lax
from jax.sharding import PartitionSpec as P

H = 48
KVH = 8
HD = 128


def combined_all(value, axis, join):
    pieces = jax.tree.map(lambda part: lax.all_gather(part, axis), value)
    head = jax.tree.map(lambda part: part[0], pieces)
    tail = jax.tree.map(lambda part: part[1:], pieces)
    running, _ = lax.scan(lambda running, share: (join(running, share), None), head, tail)
    return running


def merge_parts(earlier, later):
    high_left, total_left, sum_left = earlier
    high_right, total_right, sum_right = later
    joined = jnp.maximum(high_left, high_right)
    scale_left = jnp.exp(high_left - joined)
    scale_right = jnp.exp(high_right - joined)
    return (
        joined,
        total_left * scale_left + total_right * scale_right,
        sum_left * scale_left[..., None] + sum_right * scale_right[..., None],
    )


def partial_attention(query_rows, relaid, positions, lengths, kv_count):
    requests = lengths.shape[0]
    per_group = H // KVH
    slot_count = relaid.shape[2] // requests
    query_heads = query_rows.reshape(requests, kv_count, per_group, HD)
    key_rows = relaid[0].reshape(kv_count, HD, slot_count, requests)
    value_rows = relaid[1].reshape(kv_count, HD, slot_count, requests)
    scores = jnp.einsum(
        "rgtd,gdpr->rgtp", query_heads, key_rows, preferred_element_type=jnp.float32
    ) * (1.0 / math.sqrt(HD))
    alive_mask = (positions[None, :] < lengths[:, None])[:, None, None, :]
    highest = jnp.max(jnp.where(alive_mask, scores, -1e30), axis=-1)
    weights = jnp.where(alive_mask, jnp.exp(scores - highest[..., None]), 0.0)
    summed = jnp.einsum(
        "rgtp,gdpr->rgtd",
        weights.astype(jnp.bfloat16),
        value_rows,
        preferred_element_type=jnp.float32,
    )
    return (highest, jnp.sum(weights, axis=-1), summed)


def on_device(
    residual,
    queries,
    new_entries,
    kv_cache,
    lengths,
    routing,
    w_out,
    norm_gain,
    router,
    w_gate,
    w_up,
    w_down,
):
    requests = lengths.shape[0]
    seq_count = lax.axis_size("seq")
    core_count = lax.axis_size("expert")
    seq_index = lax.axis_index("seq")
    core_index = lax.axis_index("expert")
    half_ctx = kv_cache.shape[2] // requests
    ctx_dev = half_ctx // seq_count
    own_heads = KVH // core_count
    relaid = lax.all_to_all(kv_cache, "seq", split_axis=2, concat_axis=1, tiled=True)
    positions = core_index * half_ctx + seq_index * ctx_dev + jnp.arange(ctx_dev, dtype=jnp.int32)
    all_queries = lax.all_gather(queries, "expert", axis=1, tiled=True)
    partials = partial_attention(all_queries, relaid, positions, lengths, KVH)
    merged = combined_all(partials, ("seq", "expert"), merge_parts)
    head_start = core_index * own_heads
    highest = lax.dynamic_slice_in_dim(merged[0], head_start, own_heads, 1)
    totals = lax.dynamic_slice_in_dim(merged[1], head_start, own_heads, 1)
    summed = lax.dynamic_slice_in_dim(merged[2], head_start, own_heads, 1)
    per_group = H // KVH
    query_heads = queries.reshape(requests, own_heads, per_group, HD)
    new_keys = new_entries[0].reshape(requests, own_heads, HD)
    new_values = new_entries[1].reshape(requests, own_heads, HD).astype(jnp.float32)
    own_score = jnp.einsum(
        "rgtd,rgd->rgt", query_heads, new_keys, preferred_element_type=jnp.float32
    ) * (1.0 / math.sqrt(HD))
    joined = jnp.maximum(highest, own_score)
    fade_old = jnp.exp(highest - joined)
    own_weight = jnp.exp(own_score - joined)
    numerator = summed * fade_old[..., None] + own_weight[..., None] * new_values[:, :, None, :]
    denominator = totals * fade_old + own_weight
    attn_rows = (
        (numerator / denominator[..., None])
        .reshape(requests, own_heads * per_group * HD)
        .astype(jnp.bfloat16)
    )
    head_terms = jnp.dot(attn_rows, w_out, preferred_element_type=jnp.float32)
    attended = (residual.astype(jnp.float32) + lax.psum(head_terms, "expert")).astype(jnp.bfloat16)
    gathered = lax.all_gather(attended, "seq", axis=1, tiled=True)
    widened = gathered.astype(jnp.float32)
    mean_square = jnp.mean(widened * widened, axis=-1, keepdims=True)
    normed = (widened * lax.rsqrt(mean_square + 1e-05) * norm_gain.astype(jnp.float32)).astype(
        jnp.bfloat16
    )
    logits = jnp.dot(normed, router, preferred_element_type=jnp.float32)
    expert_total = router.shape[1]
    picked = (
        routing[:, :, None] == jnp.arange(expert_total, dtype=jnp.int32)[None, None, :]
    ).astype(jnp.float32)
    chosen = jnp.sum(picked * logits[:, None, :], axis=-1)
    first_share = jax.nn.sigmoid(chosen[:, 0] - chosen[:, 1])
    shares = jnp.stack([first_share, 1.0 - first_share], axis=-1)
    combine = jnp.sum(picked * shares[:, :, None], axis=1)
    local_ids = core_index * w_gate.shape[0] + jnp.arange(w_gate.shape[0], dtype=jnp.int32)
    select = (jnp.arange(expert_total, dtype=jnp.int32)[:, None] == local_ids[None, :]).astype(
        jnp.float32
    )
    local_share = jnp.sum(combine[:, :, None] * select[None, :, :], axis=1)
    gate_proj = jnp.einsum("rd,edf->ref", normed, w_gate, preferred_element_type=jnp.float32)
    upward = jnp.einsum("rd,edf->ref", normed, w_up, preferred_element_type=jnp.float32)
    activation = (jax.nn.silu(gate_proj) * upward * local_share[:, :, None]).astype(jnp.bfloat16)
    expert_terms = jnp.einsum("ref,efd->rd", activation, w_down, preferred_element_type=jnp.float32)
    reduced = lax.psum_scatter(expert_terms, "seq", scatter_dimension=1, tiled=True)
    expert_out = lax.psum(reduced, "expert").astype(jnp.bfloat16)
    return (attended, expert_out)


def solution(mesh):
    in_specs = (
        P("groups", "seq"),
        P("groups", "expert"),
        P(None, "groups", "expert"),
        P(None, "seq", ("groups", "expert")),
        P("groups"),
        P("groups", None),
        P("expert", "seq"),
        P(),
        P(),
        P("expert", None, "seq"),
        P("expert", None, "seq"),
        P("expert", "seq", None),
    )
    out_specs = (P("groups", "seq"), P("groups", "seq"))
    return jax.shard_map(
        on_device, mesh=mesh, in_specs=in_specs, out_specs=out_specs, check_vma=False
    )
```

profile of v0, /device:TPU:0, one launch (start us, length us, event | category | flops | bytes accessed | tf_op | source)
XLA Modules:
  0.0 286.1 jit_solution(10244432440107724800)
XLA Ops:
  7.2 6.3 %copy.89 = bf16[2,128,4096]{1,0,2:T(2,128)(2,1)} copy(bf16[2,128,4096]{2,1,0:T(8,128)(2,1)} %param.17) | data formatting | bytes 4194304 | tf_op args[3]
  13.5 7.4 %all-to-all-start = ((bf16[2,128,4096]{1,0,2:T(2,128)(2,1)}), bf16[2,128,4096]{1,0,2:T(2,128)(2,1)}, u32[]{:S(2)}, u32[]{:S(2)}) async-start(bf16[2,128,4096]{1,0,2:T(2,128)(2,1)} %copy.89), calls=%async_computation | async-start | bytes 4194304 | tf_op jit(solution)/shard_map/all_to_all | solution.py:77
  21.0 1.8 all_gather.24
  23.0 46.3 %all-to-all-done = bf16[2,128,4096]{1,0,2:T(2,128)(2,1)} async-done(((bf16[2,128,4096]{1,0,2:T(2,128)(2,1)}), bf16[2,128,4096]{1,0,2:T(2,128)(2,1)}, u32[]{:S(2)}, u32[]{:S(2)}) %all-to-all-start) | async-done | bytes 2097184 | tf_op jit(solution)/shard_map/all_to_all | solution.py:77
  69.3 1.9 copy.90
  75.6 20.3 %all-gather.1 = f32[64,8,6]{2,1,0:T(8,128)S(1)} all-gather(f32[4,8,6]{2,1,0:T(8,128)S(1)} %fusion.10), channel_id=3, replica_groups=mesh['groups'=2,'seq'=8,'expert'=2] {'seq','expert'}, dimensions={0}, use_global_device_ids=true | all-gather | bytes 13056 | tf_op jit(solution)/shard_map/all_gather | solution.py:13
  95.9 18.6 %all-gather = f32[64,8,6]{2,1,0:T(8,128)S(1)} all-gather(f32[4,8,6]{2,1,0:T(8,128)S(1)} %get-tuple-element.106), channel_id=2, replica_groups=mesh['groups'=2,'seq'=8,'expert'=2] {'seq','expert'}, dimensions={0}, use_global_device_ids=true | all-gather | bytes 13056 | tf_op jit(solution)/shard_map/all_gather | solution.py:13
  115.8 1.1 copy.102
  117.0 1.4 copy.101
  119.2 0.9 slice.60
  120.2 2.6 slice.63
  122.7 30.3 %while.14 = (s32[]{:T(128)}, f32[4,8,6]{1,0,2:T(4,128)S(1)}, f32[4,8,6]{1,0,2:T(4,128)S(1)}, f32[4,8,6,128]{3,2,1,0:T(8,128)S(1)}, f32[15,4,8,6]{2,1,3,0:T(4,128...) while((s32[]{:T(128)}, f32[4,8,6]{1,0,2:T(4,128)S(1)}, ...), condition=%wide.region_3.4_spmd, body=%wide.region_2.3_spmd.sunk | while | flops 74882 | bytes 502365 | solution.py:16
  125.7 0.9 constant_dynamic-slice_fusion.2
  131.8 0.9 constant_dynamic-slice_fusion.2
  133.8 0.9 constant_dynamic-slice_fusion.2
  141.9 0.9 constant_dynamic-slice_fusion.2
  154.9 3.1 %fusion.36 = f32[4,768]{1,0:T(4,128)S(1)} fusion(bf16[4,3072]{1,0:T(4,128)(2,1)S(1)} %convert_element_type.53, bf16[3072,768]{1,0:T(8,128)(2,1)} %param.20), kind=kOutput, calls=%fused_computation.63 | convolution fusion | flops 18874368 | bytes 4755456 | tf_op jit(solution)/shard_map/dot_general | solution.py:103
  158.0 3.5 %psum.14 = f32[4,768]{1,0:T(4,128)S(1)} all-reduce(f32[4,768]{1,0:T(4,128)S(1)} %fusion.36), channel_id=1, replica_groups=mesh['groups'=2,'seq'=8,'expert'=2] {'expert'}, use_global_device_ids=true, to_apply=%region_4.5 | all-reduce | flops 3072 | bytes 24576 | tf_op jit(solution)/shard_map/psum | solution.py:104
  161.5 30.8 %all_gather.31 = bf16[4,6144]{1,0:T(4,128)(2,1)S(1)} all-gather(bf16[4,768]{1,0:T(4,128)(2,1)S(1)} %add_convert_fusion), channel_id=1, replica_groups=mesh['groups'=2,'seq'=8,'expert'=2] {'seq'}, dimensions={1}, use_global_device_ids=true | all-gather | bytes 55296 | tf_op jit(solution)/shard_map/all_gather | solution.py:105
  193.0 2.4 fusion.20
  195.5 5.8 %convolution_bitcast_fusion = f32[6144,4]{1,0:T(8,128)} fusion(bf16[2,128,6144]{2,1,0:T(8,128)(2,1)S(1)} %copy-done, bf16[2,6144,128]{2,1,0:T(8,128)(2,1)} %param.24, bf16[4,6144]{1,0:T(4,128)(2,1)S(1)} %fusion.13, f32[4,2,128]{2,0,1:T(4,128)S(1)} %fusion.20, f32[4,2]{0,1:T(2,128)S(1)} %multiply_reduce_fusion), kind=kOutput, calls=%fused_computation.10 | convolution fusion | flops 25172992 | bytes 6443040 | tf_op jit(solution)/shard_map/ref,efd->rd/dot_general | solution.py:128
  201.3 72.9 %reduce-scatter.4.cloned.1.call-done = f32[768,4]{1,0:T(8,128)} async-done(((f32[6144,4]{1,0:T(8,128)}), f32[768,4]{1,0:T(8,128)}) %reduce-scatter.4.cloned.1.call-update) | async-done | bytes 12304
  274.2 1.1 copy.117
  275.4 3.9 %psum.15 = bf16[4,768]{1,0:T(4,128)(2,1)} all-reduce(f32[4,768]{1,0:T(4,128)S(1)} %copy.117), channel_id=1, replica_groups=mesh['groups'=2,'seq'=8,'expert'=2] {'expert'}, use_global_device_ids=true, to_apply=%region_10.11 | all-reduce | flops 3072 | bytes 18432 | tf_op jit(solution)/shard_map/psum | solution.py:130
  (134 shorter events, 35.8 us)
Async XLA Ops:
  7.2 188.3 %copy-start = (bf16[2,128,6144]{2,1,0:T(8,128)(2,1)S(1)}, bf16[2,128,6144]{2,1,0:T(8,128)(2,1)}, u32[]{:S(2)}) copy-start(bf16[2,128,6144]{2,1,0:T(8,128)(2,1)} %param.25) | copy-start | bytes 9437188
  13.5 7.5 %copy-start.1 = (bf16[4,3072]{1,0:T(4,128)(2,1)S(1)}, bf16[4,3072]{1,0:T(4,128)(2,1)}, u32[]{:S(2)}) copy-start(bf16[4,3072]{1,0:T(4,128)(2,1)} %param.15) | copy-start | bytes 73732
  13.5 9.4 %copy-start.9 = (s32[4]{0:T(128)S(1)}, s32[4]{0:T(128)}, u32[]{:S(2)}) copy-start(s32[4]{0:T(128)} %param.18) | copy-start | bytes 52
  13.5 55.8 %all-to-all-start = ((bf16[2,128,4096]{1,0,2:T(2,128)(2,1)}), bf16[2,128,4096]{1,0,2:T(2,128)(2,1)}, u32[]{:S(2)}, u32[]{:S(2)}) async-start(bf16[2,128,4096]{1,0,2:T(2,128)(2,1)} %copy.89), calls=%async_computation | async-start | bytes 4194304 | tf_op jit(solution)/shard_map/all_to_all | solution.py:77
  21.0 98.3 %all-gather.5.cloned.1.call-start = ((), (), s32[]{:S(2)}) async-start(), calls=%async_computation.2 | async-start | bytes 1671168 | tf_op jit(solution)/shard_map/all_gather | solution.py:13
  71.2 2.2 copy-start.4
  71.2 2.8 copy-start.3
  73.3 201.0 %reduce-scatter.4.cloned.1.call-start = ((), (), s32[]{:S(2)}) async-start(), calls=%async_computation.3 | async-start | bytes 3538944
  153.1 8.3 %copy-start.5 = (bf16[4,768]{1,0:T(4,128)(2,1)S(1)}, bf16[4,768]{1,0:T(4,128)(2,1)}, u32[]{:S(2)}) copy-start(bf16[4,768]{1,0:T(4,128)(2,1)} %param.14) | copy-start | bytes 18436
  153.1 39.4 %copy-start.8 = (bf16[6144,4]{0,1:T(4,128)(2,1)S(1)}, bf16[6144,4]{0,1:T(4,128)(2,1)}, u32[]{:S(2)}) copy-start(bf16[6144,4]{0,1:T(4,128)(2,1)} %param.22) | copy-start | bytes 147460
  153.1 39.6 %copy-start.6 = (s32[4,2]{0,1:T(2,128)S(1)}, s32[4,2]{0,1:T(2,128)}, u32[]{:S(2)}) copy-start(s32[4,2]{0,1:T(2,128)} %param.19) | copy-start | bytes 100
  154.9 40.5 %copy-start.7 = (f32[4,2]{0,1:T(2,128)S(1)}, f32[4,2]{0,1:T(2,128)}, u32[]{:S(2)}) copy-start(f32[4,2]{0,1:T(2,128)} %compare_convert_fusion) | copy-start | bytes 100
  161.4 39.9 %copy-start.2 = (bf16[4,768]{1,0:T(4,128)(2,1)}, bf16[4,768]{1,0:T(4,128)(2,1)S(1)}, u32[]{:S(2)}) copy-start(bf16[4,768]{1,0:T(4,128)(2,1)S(1)} %add_convert_fusion) | copy-start | bytes 18436
Sparse Core Ops, SparseCore 0:
  73.4 39.7 all-gather.4
  201.5 72.7 reduce-scatter.3
where the time goes:
time: 288 us; the launch traced here: 286 us
  waiting for transfers between devices  119 us (41%)
  blocking collectives  78.8 us (27%)
  local copies, waits for them, and re-layouts  35.9 us (12%)
  other arithmetic  16.7 us (6%)
  between operations  14.3 us (5%)
  matrix products  13.4 us (5%)
  starting transfers between devices  7.52 us (3%)
    unnamed x3, waiting for transfers between devices  72.9 us
    all_to_all x1, waiting for transfers between devices, on_device(): lax.all_to_all(kv_cache, 'seq', split_axis=2, concat_axis=1, tiled=True)  46.3 us
    all_gather x2, blocking collectives, combined_all(): pieces = jax.tree.map(lambda part: lax.all_gather(part, axis), value)  38.9 us
    all_gather x1, blocking collectives, on_device(): gathered = lax.all_gather(attended, 'seq', axis=1, tiled=True)  30.8 us
    dynamic_slice x15, local copies, waits for them, and re-layouts, combined_all(): lax.scan(lambda running, share: (join(running, share), None), head, tail)  13.5 us
    add x15, other arithmetic, merge_parts(): total_left * scale_left + total_right * scale_right  11.2 us
    unnamed x22, local copies, waits for them, and re-layouts  7.55 us
    all_to_all x1, starting transfers between devices, on_device(): lax.all_to_all(kv_cache, 'seq', split_axis=2, concat_axis=1, tiled=True)  7.44 us
  transfers between devices with their start and end apart: 3, of which 2 were waited for; matrix products, arithmetic and copies ran while one was open for 2% of the time, Pallas kernels for 0%

commit v1 on v0

--- a/solution.py
+++ b/solution.py
@@ -74,7 +74,10 @@
     half_ctx = kv_cache.shape[2] // requests
     ctx_dev = half_ctx // seq_count
     own_heads = KVH // core_count
-    relaid = lax.all_to_all(kv_cache, "seq", split_axis=2, concat_axis=1, tiled=True)
+    relaid = jnp.concatenate(
+        lax.all_to_all(jnp.stack(jnp.split(kv_cache, lax.axis_size("seq"), axis=2)), "seq", 0, 0),
+        axis=1,
+    )
     positions = core_index * half_ctx + seq_index * ctx_dev + jnp.arange(ctx_dev, dtype=jnp.int32)
     all_queries = lax.all_gather(queries, "expert", axis=1, tiled=True)
     partials = partial_attention(all_queries, relaid, positions, lengths, KVH)

time: 288 us -> 304 us (1.056)
  local copies, waits for them, and re-layouts: 35.9 us -> 49 us
    unnamed x22 -> x28, local copies, waits for them, and re-layouts: 7.55 us -> 13.1 us
    slice x1 -> x2, local copies, waits for them, and re-layouts: 0.19 us -> 5.47 us  [partial_attention(): value_rows = relaid[1].reshape(kv_count, HD, slot_count, requests)]
where the time goes in v1:
time: 304 us; the launch traced here: 302 us
  waiting for transfers between devices  119 us (39%)
  blocking collectives  79 us (26%)
  local copies, waits for them, and re-layouts  49 us (16%)
  other arithmetic  16.7 us (5%)
  matrix products  15.9 us (5%)
  between operations  14.3 us (5%)
  starting transfers between devices  7.52 us (2%)
    unnamed x3, waiting for transfers between devices  73 us
    all_to_all x1, waiting for transfers between devices, on_device(): lax.all_to_all(jnp.stack(jnp.split(kv_cache, lax.axis_size('seq'), axis=2...  46.3 us
    all_gather x2, blocking collectives, combined_all(): pieces = jax.tree.map(lambda part: lax.all_gather(part, axis), value)  38.9 us
    all_gather x1, blocking collectives, on_device(): gathered = lax.all_gather(attended, 'seq', axis=1, tiled=True)  30.8 us
    dynamic_slice x15, local copies, waits for them, and re-layouts, combined_all(): lax.scan(lambda running, share: (join(running, share), None), head, tail)  13.5 us
    unnamed x28, local copies, waits for them, and re-layouts  13.1 us
    add x15, other arithmetic, merge_parts(): total_left * scale_left + total_right * scale_right  11.2 us
    all_to_all x1, starting transfers between devices, on_device(): lax.all_to_all(jnp.stack(jnp.split(kv_cache, lax.axis_size('seq'), axis=2...  7.44 us
  transfers between devices with their start and end apart: 3, of which 2 were waited for; matrix products, arithmetic and copies ran while one was open for 2% of the time, Pallas kernels for 0%

profile of v1, /device:TPU:0, one launch (start us, length us, event | category | flops | bytes accessed | tf_op | source)
XLA Modules:
  0.0 301.9 jit_solution(11657298042880161934)
XLA Ops:
  7.2 1.8 bitcast_dynamic-update-slice_fusion.7
  12.4 1.7 bitcast_dynamic-update-slice_fusion.4
  14.0 1.7 bitcast_dynamic-update-slice_fusion.3
  15.7 1.7 bitcast_dynamic-update-slice_fusion.2
  19.1 1.7 bitcast_dynamic-update-slice_fusion
  20.7 7.4 %all-to-all-start = ((bf16[8,2,128,512]{3,2,1,0:T(8,128)(2,1)}), bf16[8,2,128,512]{3,2,1,0:T(8,128)(2,1)}, u32[]{:S(2)}, u32[]{:S(2)}) async-start(bf16[8,2,128,512]{3,2,1,0:T(8,128)(2,1)} %bitcast_dynamic-update-slice_fusion), calls=%async_computation | async-start | bytes 4194304 | tf_op jit(solution)/shard_map/all_to_all | solution.py:78
  28.3 1.8 all_gather.24
  30.3 46.3 %all-to-all-done = bf16[8,2,128,512]{3,2,1,0:T(8,128)(2,1)} async-done(((bf16[8,2,128,512]{3,2,1,0:T(8,128)(2,1)}), bf16[8,2,128,512]{3,2,1,0:T(8,128)(2,1)}, u32[]{:S(2)}, u32[]{:S(2)}) %all-to-all-start) | async-done | bytes 2097184 | tf_op jit(solution)/shard_map/all_to_all | solution.py:78
  76.5 3.0 %fusion.31 = (bf16[1,8,128,512]{3,2,0,1:T(8,128)(2,1)}, bf16[1,8,128,512]{3,2,0,1:T(8,128)(2,1)}) fusion(bf16[2,8,128,512]{3,2,0,1:T(8,128)(2,1)} %bitcast.11), kind=kLoop, calls=%fused_computation.69 | loop fusion | bytes 4194304 | tf_op jit(solution)/shard_map/slice | solution.py:39
  79.6 2.4 copy.92
  82.0 2.4 copy.94
  84.5 2.0 select_reduce_fusion
  86.4 1.7 fusion.6
  91.2 20.3 %all-gather.1 = f32[64,8,6]{2,1,0:T(8,128)S(1)} all-gather(f32[4,8,6]{2,1,0:T(8,128)S(1)} %bitcast_reduce_fusion), channel_id=3, replica_groups=mesh['groups'=2,'seq'=8,'expert'=2] {'seq','expert'}, dimensions={0}, use_global_device_ids=true | all-gather | bytes 13056 | tf_op jit(solution)/shard_map/all_gather | solution.py:13
  111.5 18.6 %all-gather = f32[64,8,6]{2,1,0:T(8,128)S(1)} all-gather(f32[4,8,6]{2,1,0:T(8,128)S(1)} %get-tuple-element.106), channel_id=2, replica_groups=mesh['groups'=2,'seq'=8,'expert'=2] {'seq','expert'}, dimensions={0}, use_global_device_ids=true | all-gather | bytes 13056 | tf_op jit(solution)/shard_map/all_gather | solution.py:13
  135.7 2.6 slice.63
  138.3 30.3 %while.14 = (s32[]{:T(128)}, f32[4,8,6]{1,0,2:T(4,128)S(1)}, f32[4,8,6]{1,0,2:T(4,128)S(1)}, f32[4,8,6,128]{3,2,1,0:T(8,128)S(1)}, f32[15,4,8,6]{2,1,3,0:T(4,128...) while((s32[]{:T(128)}, f32[4,8,6]{1,0,2:T(4,128)S(1)}, ...), condition=%wide.region_3.4_spmd, body=%wide.region_2.3_spmd.sunk | while | flops 74882 | bytes 502365 | solution.py:16
  170.5 3.1 %fusion.33 = f32[4,768]{1,0:T(4,128)S(1)} fusion(bf16[4,3072]{1,0:T(4,128)(2,1)S(1)} %convert_element_type.53, bf16[3072,768]{1,0:T(8,128)(2,1)} %param.20), kind=kOutput, calls=%fused_computation.71 | convolution fusion | flops 18874368 | bytes 4755456 | tf_op jit(solution)/shard_map/dot_general | solution.py:106
  173.5 3.6 %psum.14 = f32[4,768]{1,0:T(4,128)S(1)} all-reduce(f32[4,768]{1,0:T(4,128)S(1)} %fusion.33), channel_id=1, replica_groups=mesh['groups'=2,'seq'=8,'expert'=2] {'expert'}, use_global_device_ids=true, to_apply=%region_4.5 | all-reduce | flops 3072 | bytes 24576 | tf_op jit(solution)/shard_map/psum | solution.py:107
  177.2 30.8 %all_gather.31 = bf16[4,6144]{1,0:T(4,128)(2,1)S(1)} all-gather(bf16[4,768]{1,0:T(4,128)(2,1)S(1)} %add_convert_fusion), channel_id=1, replica_groups=mesh['groups'=2,'seq'=8,'expert'=2] {'seq'}, dimensions={1}, use_global_device_ids=true | all-gather | bytes 55296 | tf_op jit(solution)/shard_map/all_gather | solution.py:108
  208.7 2.4 fusion.17
  211.2 5.8 %convolution_bitcast_fusion = f32[6144,4]{1,0:T(8,128)} fusion(bf16[2,128,6144]{2,1,0:T(8,128)(2,1)S(1)} %copy-done, bf16[2,6144,128]{2,1,0:T(8,128)(2,1)} %param.24, bf16[4,6144]{1,0:T(4,128)(2,1)S(1)} %fusion.11, f32[4,2,128]{2,0,1:T(4,128)S(1)} %fusion.17, f32[4,2]{0,1:T(2,128)S(1)} %multiply_reduce_fusion), kind=kOutput, calls=%fused_computation.10 | convolution fusion | flops 25172992 | bytes 6443040 | tf_op jit(solution)/shard_map/ref,efd->rd/dot_general | solution.py:131
  217.1 72.9 %reduce-scatter.4.cloned.1.call-done = f32[768,4]{1,0:T(8,128)} async-done(((f32[6144,4]{1,0:T(8,128)}), f32[768,4]{1,0:T(8,128)}) %reduce-scatter.4.cloned.1.call-update) | async-done | bytes 12304
  291.1 3.9 %psum.15 = bf16[4,768]{1,0:T(4,128)(2,1)} all-reduce(f32[4,768]{1,0:T(4,128)S(1)} %copy.114), channel_id=1, replica_groups=mesh['groups'=2,'seq'=8,'expert'=2] {'expert'}, use_global_device_ids=true, to_apply=%region_10.11 | all-reduce | flops 3072 | bytes 18432 | tf_op jit(solution)/shard_map/psum | solution.py:133
  (142 shorter events, 47.6 us)
Async XLA Ops:
  7.2 204.0 %copy-start = (bf16[2,128,6144]{2,1,0:T(8,128)(2,1)S(1)}, bf16[2,128,6144]{2,1,0:T(8,128)(2,1)}, u32[]{:S(2)}) copy-start(bf16[2,128,6144]{2,1,0:T(8,128)(2,1)} %param.25) | copy-start | bytes 9437188
  20.7 7.5 %copy-start.1 = (bf16[4,3072]{1,0:T(4,128)(2,1)S(1)}, bf16[4,3072]{1,0:T(4,128)(2,1)}, u32[]{:S(2)}) copy-start(bf16[4,3072]{1,0:T(4,128)(2,1)} %param.15) | copy-start | bytes 73732
  20.7 9.4 %copy-start.9 = (s32[4]{0:T(128)S(1)}, s32[4]{0:T(128)}, u32[]{:S(2)}) copy-start(s32[4]{0:T(128)} %param.18) | copy-start | bytes 52
  20.7 55.8 %all-to-all-start = ((bf16[8,2,128,512]{3,2,1,0:T(8,128)(2,1)}), bf16[8,2,128,512]{3,2,1,0:T(8,128)(2,1)}, u32[]{:S(2)}, u32[]{:S(2)}) async-start(bf16[8,2,128,512]{3,2,1,0:T(8,128)(2,1)} %bitcast_dynamic-update-slice_fusion), calls=%async_computation | async-start | bytes 4194304 | tf_op jit(solution)/shard_map/all_to_all | solution.py:78
  28.2 106.6 %all-gather.5.cloned.1.call-start = ((), (), s32[]{:S(2)}) async-start(), calls=%async_computation.2 | async-start | bytes 1671168 | tf_op jit(solution)/shard_map/all_gather | solution.py:13
  84.4 4.5 %copy-start.4 = (bf16[2,4,512]{2,1,0:T(4,128)(2,1)S(1)}, bf16[2,4,512]{2,1,0:T(4,128)(2,1)}, u32[]{:S(2)}) copy-start(bf16[2,4,512]{2,1,0:T(4,128)(2,1)} %param.16) | copy-start | bytes 24580
  84.4 5.1 %copy-start.3 = (bf16[6144]{0:T(1024)(128)(2,1)S(1)}, bf16[6144]{0:T(1024)(128)(2,1)}, u32[]{:S(2)}) copy-start(bf16[6144]{0:T(1024)(128)(2,1)} %param.21) | copy-start | bytes 36868
  88.8 201.2 %reduce-scatter.4.cloned.1.call-start = ((), (), s32[]{:S(2)}) async-start(), calls=%async_computation.3 | async-start | bytes 3538944
  170.4 6.7 %copy-start.5 = (bf16[4,768]{1,0:T(4,128)(2,1)S(1)}, bf16[4,768]{1,0:T(4,128)(2,1)}, u32[]{:S(2)}) copy-start(bf16[4,768]{1,0:T(4,128)(2,1)} %param.14) | copy-start | bytes 18436
  170.4 37.8 %copy-start.8 = (bf16[6144,4]{0,1:T(4,128)(2,1)S(1)}, bf16[6144,4]{0,1:T(4,128)(2,1)}, u32[]{:S(2)}) copy-start(bf16[6144,4]{0,1:T(4,128)(2,1)} %param.22) | copy-start | bytes 147460
  170.5 37.9 %copy-start.6 = (s32[4,2]{0,1:T(2,128)S(1)}, s32[4,2]{0,1:T(2,128)}, u32[]{:S(2)}) copy-start(s32[4,2]{0,1:T(2,128)} %param.19) | copy-start | bytes 100
  173.5 37.5 %copy-start.7 = (f32[4,2]{0,1:T(2,128)S(1)}, f32[4,2]{0,1:T(2,128)}, u32[]{:S(2)}) copy-start(f32[4,2]{0,1:T(2,128)} %compare_convert_fusion) | copy-start | bytes 100
  177.2 39.9 %copy-start.2 = (bf16[4,768]{1,0:T(4,128)(2,1)}, bf16[4,768]{1,0:T(4,128)(2,1)S(1)}, u32[]{:S(2)}) copy-start(bf16[4,768]{1,0:T(4,128)(2,1)S(1)} %add_convert_fusion) | copy-start | bytes 18436
Sparse Core Ops, SparseCore 0:
  89.0 39.7 all-gather.4
  217.2 72.7 reduce-scatter.3
